TPU v7x, 32 devices: a whole 2x2x4 slice. The times are simulated.
32 devices in a mesh: dp: 4 (over x, core), wide: 8 (over z, y).
Axes of the slice: x: 2, y: 2, z: 4, core: 2. Of those that a mesh axis runs over, the one named last changes fastest.
Arguments:
- streams: float32 [4, 4096, 2048], P(None, 'dp', 'wide'), may hold values from -8 to 8
- cotangent: float32 [4, 4096, 2048], P(None, 'dp', 'wide'), may hold values from -6 to 6
- w_query: bfloat16 [2048, 2048], P('dp', 'wide'), may hold values from -2 to 2
- w_key: bfloat16 [2048, 2048], P('dp', 'wide'), may hold values from -0.125 to 0.125
- w_value: bfloat16 [2048, 2048], P('dp', 'wide'), may hold values from -0.125 to 0.125
- w_out: bfloat16 [2048, 2048], P('wide', 'dp'), may hold values from -1 to 1
- w_gate: bfloat16 [2048, 8192], P('dp', 'wide'), may hold values from -0.125 to 0.125
- w_up: bfloat16 [2048, 8192], P('dp', 'wide'), may hold values from -0.125 to 0.125
- w_down: bfloat16 [8192, 2048], P('wide', 'dp'), may hold values from -0.0625 to 0.0625
- hyper: float32 [2, 4, 6], replicated, may hold values from 0.1 to 0.6
- doc_ids: int32 [4, 1024], P('dp'), may hold values from 0 to 3, never falling along the last dimension, each value on 1 to 512 neighbouring positions
- span_starts: int32 [4, 2], P('dp'), may hold values from 0 to 768, as said below
- span_lengths: int32 [4, 2], P('dp'), may hold values from 64 to 256
Outputs:
- out_streams: float32 [4, 4096, 2048], P(None, 'dp', 'wide')
- d_streams: float32 [4, 4096, 2048], P(None, 'dp', 'wide')
- grad_query: float32 [2048, 2048], P('dp', 'wide')
- grad_key: float32 [2048, 2048], P('dp', 'wide')
- grad_value: float32 [2048, 2048], P('dp', 'wide')
- grad_out: float32 [2048, 2048], P('wide', 'dp')
- grad_gate: float32 [2048, 8192], P('dp', 'wide')
- grad_up: float32 [2048, 8192], P('dp', 'wide')
- grad_down: float32 [8192, 2048], P('wide', 'dp')
- grad_hyper: float32 [2, 4, 6], replicated
- clip_scale: float32 [16], P('wide')
- query_clipped: float32 [2048, 2048], P('dp', 'wide')
- key_clipped: float32 [2048, 2048], P('dp', 'wide')
Inputs may be any that keep to these rules, and one draw needn't show every extreme that they name: `doc_ids`: each row's document numbers never fall; every document holds 1 to 512 tokens, and one holds exactly 512. `span_starts`: span k of a sequence starts and ends inside the k-th of 2 equal regions of the sequence.
All inputs are finite; a program needn't handle non-finite values.
Results may differ from a plain program's by a relative error of at most 0.018.
Values may be sent and summed in bfloat16 or wider, within the bound.
A program may use at most 192 MiB of HBM per device.

v0:
```python
import math
import jax
import jax.numpy as jnp
from jax import lax
from jax.sharding import PartitionSpec as P

D = 2048
H = 16
CLIP_TAU = 6
EPSILON = 1e-05
MASKED = -1e30


def rope_tables(length, head_size):
    half_size = head_size // 2
    inverse = 10000.0 ** (-2.0 * jnp.arange(half_size, dtype=jnp.float32) / head_size)
    angles = jnp.arange(length, dtype=jnp.float32)[:, None] * inverse[None, :]
    cosine_table = jnp.cos(angles)
    sine_table = jnp.sin(angles)
    return (
        jnp.concatenate([cosine_table, cosine_table], axis=1),
        jnp.concatenate([sine_table, sine_table], axis=1),
    )


def rotate(values, cosine_table, sine_table):
    half_size = values.shape[-1] // 2
    turned = jnp.concatenate([-values[..., half_size:], values[..., :half_size]], axis=-1)
    return values * cosine_table[:, None, :] + turned * sine_table[:, None, :]


def rotate_back(grads, cosine_table, sine_table):
    half_size = grads.shape[-1] // 2
    scaled = grads * sine_table[:, None, :]
    turned = jnp.concatenate([scaled[..., half_size:], -scaled[..., :half_size]], axis=-1)
    return grads * cosine_table[:, None, :] + turned


def mix_inputs(weights_in, stream_set):
    return jnp.sum(weights_in[:, None, None] * stream_set, axis=0)


def mix_streams(matrix, stream_set):
    return jnp.sum(matrix[:, :, None, None] * stream_set[None, :, :, :], axis=1)


def mix_back(matrix, grads):
    return jnp.sum(matrix[:, :, None, None] * grads[:, None, :, :], axis=0)


def hyper_rows(pre_grad, post_grad, mix_grad):
    return jnp.concatenate([pre_grad[:, None], post_grad[:, None], mix_grad], axis=1)


def span_labels(positions, starts, lengths):
    inside = (positions[:, None] >= starts[None, :]) & (
        positions[:, None] < (starts + lengths)[None, :]
    )
    numbers = jnp.arange(1, starts.shape[0] + 1, dtype=jnp.int32)
    return jnp.sum(jnp.where(inside, numbers[None, :], 0), axis=1)


def block_mask(doc_row, labels, start_row, count_rows):
    key_pos = jnp.arange(doc_row.shape[0], dtype=jnp.int32)
    query_pos = start_row + jnp.arange(count_rows, dtype=jnp.int32)
    query_docs = lax.dynamic_slice_in_dim(doc_row, start_row, count_rows)
    query_labels = lax.dynamic_slice_in_dim(labels, start_row, count_rows)
    same_doc = query_docs[:, None] == doc_row[None, :]
    causal = key_pos[None, :] <= query_pos[:, None]
    joint_span = (query_labels[:, None] > 0) & (query_labels[:, None] == labels[None, :])
    return same_doc & (causal | joint_span)


def attend_forward(queries, keys_roped, values, doc_row, starts, lengths, score_scale):
    length, head_count, head_size = queries.shape
    block_rows = min(512, length)
    labels = span_labels(jnp.arange(length, dtype=jnp.int32), starts, lengths)

    def one_block(block_index):
        start_row = block_index * block_rows
        query_rows = lax.dynamic_slice_in_dim(queries, start_row, block_rows, 0)
        scores = (
            jnp.einsum("qhd,khd->hqk", query_rows, keys_roped, preferred_element_type=jnp.float32)
            * score_scale
        )
        allowed = block_mask(doc_row, labels, start_row, block_rows)
        masked = jnp.where(allowed[None, :, :], scores, MASKED)
        largest = jnp.max(masked, axis=2)
        exponent = jnp.exp(masked - largest[:, :, None])
        totals = jnp.sum(exponent, axis=2)
        weights_low = (exponent / totals[:, :, None]).astype(jnp.bfloat16)
        attended = jnp.einsum(
            "hqk,khd->qhd", weights_low, values, preferred_element_type=jnp.float32
        )
        return (attended, largest + jnp.log(totals), jnp.max(largest, axis=1))

    attended, log_sums, block_tops = lax.map(
        one_block, jnp.arange(length // block_rows, dtype=jnp.int32)
    )
    return (attended.reshape(length, head_count, head_size), log_sums, jnp.max(block_tops, axis=0))


def attend_backward(
    queries, keys_roped, values, dout, log_sums, doc_row, starts, lengths, score_scale
):
    length, head_count, head_size = queries.shape
    block_rows = min(512, length)
    labels = span_labels(jnp.arange(length, dtype=jnp.int32), starts, lengths)

    def one_block(carry, inputs):
        key_grad, value_grad = carry
        block_index, log_rows = inputs
        start_row = block_index * block_rows
        query_rows = lax.dynamic_slice_in_dim(queries, start_row, block_rows, 0)
        dout_rows = lax.dynamic_slice_in_dim(dout, start_row, block_rows, 0)
        scores = (
            jnp.einsum("qhd,khd->hqk", query_rows, keys_roped, preferred_element_type=jnp.float32)
            * score_scale
        )
        allowed = block_mask(doc_row, labels, start_row, block_rows)
        masked = jnp.where(allowed[None, :, :], scores, MASKED)
        weights_full = jnp.where(allowed[None, :, :], jnp.exp(masked - log_rows[:, :, None]), 0.0)
        weight_grad = jnp.einsum(
            "qhd,khd->hqk", dout_rows, values, preferred_element_type=jnp.float32
        )
        centre = jnp.sum(weights_full * weight_grad, axis=2, keepdims=True)
        score_grad = (weights_full * (weight_grad - centre)).astype(jnp.bfloat16)
        query_grad = score_scale * jnp.einsum(
            "hqk,khd->qhd", score_grad, keys_roped, preferred_element_type=jnp.float32
        )
        key_grad = key_grad + score_scale * jnp.einsum(
            "hqk,qhd->khd", score_grad, query_rows, preferred_element_type=jnp.float32
        )
        value_grad = value_grad + jnp.einsum(
            "hqk,qhd->khd",
            weights_full.astype(jnp.bfloat16),
            dout_rows,
            preferred_element_type=jnp.float32,
        )
        return ((key_grad, value_grad), query_grad)

    empty_grad = jnp.zeros((length, head_count, head_size), jnp.float32)
    count_blocks = length // block_rows
    (key_grad, value_grad), query_grad = lax.scan(
        one_block, (empty_grad, empty_grad), (jnp.arange(count_blocks, dtype=jnp.int32), log_sums)
    )
    return (query_grad.reshape(length, head_count, head_size), key_grad, value_grad)


def row_sums(first_term, second_term):
    return lax.psum((jnp.sum(first_term, axis=1), jnp.sum(second_term, axis=1)), "wide")


def features(piece):
    return lax.all_gather(piece, "wide", axis=1, tiled=True)


def branch_rows(partial_value):
    return lax.psum_scatter(partial_value, "wide", scatter_dimension=1, tiled=True)


def norm_forward(hidden):
    local_width = hidden.shape[1]
    full_width = local_width * lax.axis_size("wide")
    row_total, squares = row_sums(hidden, hidden * hidden)
    centre = row_total / full_width
    spread = squares / full_width - centre * centre
    inverse = lax.rsqrt(spread + EPSILON)
    normed = (hidden - centre[:, None]) * inverse[:, None]
    return (features(normed.astype(jnp.bfloat16)), normed, inverse)


def norm_backward(partial_value, normed, inverse):
    full_width = partial_value.shape[1]
    grad_rows = lax.psum_scatter(partial_value, "wide", scatter_dimension=1, tiled=True)
    row_total, row_cross = row_sums(grad_rows, grad_rows * normed)
    return inverse[:, None] * (
        grad_rows - row_total[:, None] / full_width - normed * row_cross[:, None] / full_width
    )


def per_device(
    streams,
    cotangent,
    w_query,
    w_key,
    w_value,
    w_out,
    w_gate,
    w_up,
    w_down,
    hyper,
    doc_ids,
    span_starts,
    span_lengths,
):
    seq_count, length = doc_ids.shape
    tokens = streams.shape[1]
    head_size = D // H
    column_count = w_query.shape[1]
    head_count = column_count // head_size
    score_scale = 1.0 / math.sqrt(head_size)
    cosine_table, sine_table = rope_tables(length, head_size)
    shape_heads = (seq_count, length, head_count, head_size)
    attn_pre, attn_post, attn_mix = (hyper[0, :, 0], hyper[0, :, 1], hyper[0, :, 2:])
    ffn_pre, ffn_post, ffn_mix = (hyper[1, :, 0], hyper[1, :, 1], hyper[1, :, 2:])
    query_w, key_w, value_w, out_w = (
        lax.all_gather(w_query, "dp", axis=0, tiled=True),
        lax.all_gather(w_key, "dp", axis=0, tiled=True),
        lax.all_gather(w_value, "dp", axis=0, tiled=True),
        lax.all_gather(w_out, "dp", axis=1, tiled=True),
    )
    gate_w, up_w, down_w = (
        lax.all_gather(w_gate, "dp", axis=0, tiled=True),
        lax.all_gather(w_up, "dp", axis=0, tiled=True),
        lax.all_gather(w_down, "dp", axis=1, tiled=True),
    )
    normed_one, kept_one, inverse_one = norm_forward(mix_inputs(attn_pre, streams))
    query_raw = jnp.dot(normed_one, query_w, preferred_element_type=jnp.float32).reshape(
        shape_heads
    )
    key_raw = jnp.dot(normed_one, key_w, preferred_element_type=jnp.float32).reshape(shape_heads)
    values = (
        jnp.dot(normed_one, value_w, preferred_element_type=jnp.float32)
        .astype(jnp.bfloat16)
        .reshape(shape_heads)
    )
    queries = rotate(query_raw, cosine_table, sine_table).astype(jnp.bfloat16)
    keys_roped = rotate(key_raw, cosine_table, sine_table).astype(jnp.bfloat16)

    def forward_sequence(inputs):
        return attend_forward(
            inputs[0], inputs[1], inputs[2], inputs[3], inputs[4], inputs[5], score_scale
        )

    attended, log_sums, seq_tops = lax.map(
        forward_sequence, (queries, keys_roped, values, doc_ids, span_starts, span_lengths)
    )
    head_top = lax.pmax(jnp.max(seq_tops, axis=0), "dp")
    attended_low = attended.reshape(tokens, column_count).astype(jnp.bfloat16)
    branch_one = branch_rows(jnp.dot(attended_low, out_w, preferred_element_type=jnp.float32))
    after_attn = mix_streams(attn_mix, streams) + attn_post[:, None, None] * branch_one[None, :, :]
    normed_two, kept_two, inverse_two = norm_forward(mix_inputs(ffn_pre, after_attn))
    gate_proj = jnp.dot(normed_two, gate_w, preferred_element_type=jnp.float32)
    up_proj = jnp.dot(normed_two, up_w, preferred_element_type=jnp.float32)
    sigmoid_gate = jax.nn.sigmoid(gate_proj)
    hidden = (gate_proj * sigmoid_gate * up_proj).astype(jnp.bfloat16)
    branch_two = branch_rows(jnp.dot(hidden, down_w, preferred_element_type=jnp.float32))
    out_streams = (
        mix_streams(ffn_mix, after_attn) + ffn_post[:, None, None] * branch_two[None, :, :]
    )
    ffn_post_grad = jnp.sum(cotangent * branch_two[None, :, :], axis=(1, 2))
    ffn_mix_grad = jnp.sum(cotangent[:, None, :, :] * after_attn[None, :, :, :], axis=(2, 3))
    two_grad = features(jnp.sum(ffn_post[:, None, None] * cotangent, axis=0).astype(jnp.bfloat16))
    hidden_grad = jnp.dot(two_grad, down_w.T, preferred_element_type=jnp.float32)
    down_wgrad = jnp.einsum("tf,td->fd", hidden, two_grad, preferred_element_type=jnp.float32)
    gate_grad = (
        hidden_grad * up_proj * sigmoid_gate * (1.0 + gate_proj * (1.0 - sigmoid_gate))
    ).astype(jnp.bfloat16)
    up_grad = (hidden_grad * gate_proj * sigmoid_gate).astype(jnp.bfloat16)
    gate_wgrad = jnp.einsum("td,tf->df", normed_two, gate_grad, preferred_element_type=jnp.float32)
    up_wgrad = jnp.einsum("td,tf->df", normed_two, up_grad, preferred_element_type=jnp.float32)
    gate_shard, up_shard, down_shard = (
        lax.psum_scatter(gate_wgrad, "dp", scatter_dimension=0, tiled=True),
        lax.psum_scatter(up_wgrad, "dp", scatter_dimension=0, tiled=True),
        lax.psum_scatter(down_wgrad, "dp", scatter_dimension=1, tiled=True),
    )
    normed_two_grad = jnp.dot(gate_grad, gate_w.T, preferred_element_type=jnp.float32) + jnp.dot(
        up_grad, up_w.T, preferred_element_type=jnp.float32
    )
    h_two_grad = norm_backward(normed_two_grad, kept_two, inverse_two)
    ffn_pre_grad = jnp.sum(h_two_grad[None, :, :] * after_attn, axis=(1, 2))
    after_grad = mix_back(ffn_mix, cotangent) + ffn_pre[:, None, None] * h_two_grad[None, :, :]
    attn_post_grad = jnp.sum(after_grad * branch_one[None, :, :], axis=(1, 2))
    attn_mix_grad = jnp.sum(after_grad[:, None, :, :] * streams[None, :, :, :], axis=(2, 3))
    one_grad = features(jnp.sum(attn_post[:, None, None] * after_grad, axis=0).astype(jnp.bfloat16))
    attended_grad = jnp.dot(one_grad, out_w.T, preferred_element_type=jnp.float32).astype(
        jnp.bfloat16
    )
    out_wgrad = jnp.einsum("tc,td->cd", attended_low, one_grad, preferred_element_type=jnp.float32)

    def backward_sequence(inputs):
        return attend_backward(
            inputs[0],
            inputs[1],
            inputs[2],
            inputs[3],
            inputs[4],
            inputs[5],
            inputs[6],
            inputs[7],
            score_scale,
        )

    query_grad, key_grad, value_grad = lax.map(
        backward_sequence,
        (
            queries,
            keys_roped,
            values,
            attended_grad.reshape(shape_heads),
            log_sums,
            doc_ids,
            span_starts,
            span_lengths,
        ),
    )
    query_low = (
        rotate_back(query_grad, cosine_table, sine_table)
        .reshape(tokens, column_count)
        .astype(jnp.bfloat16)
    )
    key_low = (
        rotate_back(key_grad, cosine_table, sine_table)
        .reshape(tokens, column_count)
        .astype(jnp.bfloat16)
    )
    value_low = value_grad.reshape(tokens, column_count).astype(jnp.bfloat16)
    query_wgrad = jnp.einsum("td,tc->dc", normed_one, query_low, preferred_element_type=jnp.float32)
    key_wgrad = jnp.einsum("td,tc->dc", normed_one, key_low, preferred_element_type=jnp.float32)
    value_wgrad = jnp.einsum("td,tc->dc", normed_one, value_low, preferred_element_type=jnp.float32)
    normed_one_grad = (
        jnp.dot(query_low, query_w.T, preferred_element_type=jnp.float32)
        + jnp.dot(key_low, key_w.T, preferred_element_type=jnp.float32)
        + jnp.dot(value_low, value_w.T, preferred_element_type=jnp.float32)
    )
    h_one_grad = norm_backward(normed_one_grad, kept_one, inverse_one)
    attn_pre_grad = jnp.sum(h_one_grad[None, :, :] * streams, axis=(1, 2))
    streams_grad = mix_back(attn_mix, after_grad) + attn_pre[:, None, None] * h_one_grad[None, :, :]
    hyper_grad = lax.psum(
        jnp.stack(
            [
                hyper_rows(attn_pre_grad, attn_post_grad, attn_mix_grad),
                hyper_rows(ffn_pre_grad, ffn_post_grad, ffn_mix_grad),
            ]
        ),
        ("dp", "wide"),
    )
    query_shard, key_shard, value_shard, out_shard = (
        lax.psum_scatter(query_wgrad, "dp", scatter_dimension=0, tiled=True),
        lax.psum_scatter(key_wgrad, "dp", scatter_dimension=0, tiled=True),
        lax.psum_scatter(value_wgrad, "dp", scatter_dimension=0, tiled=True),
        lax.psum_scatter(out_wgrad, "dp", scatter_dimension=1, tiled=True),
    )
    clip_scale = jnp.sqrt(CLIP_TAU / jnp.maximum(head_top, CLIP_TAU))
    columns = jnp.repeat(clip_scale, head_size)[None, :]
    return (
        out_streams,
        streams_grad,
        query_shard,
        key_shard,
        value_shard,
        out_shard,
        gate_shard,
        up_shard,
        down_shard,
        hyper_grad,
        clip_scale,
        w_query.astype(jnp.float32) * columns,
        w_key.astype(jnp.float32) * columns,
    )


def solution(mesh):
    return jax.shard_map(
        per_device,
        mesh=mesh,
        in_specs=(
            P(None, "dp", "wide"),
            P(None, "dp", "wide"),
            P("dp", "wide"),
            P("dp", "wide"),
            P("dp", "wide"),
            P("wide", "dp"),
            P("dp", "wide"),
            P("dp", "wide"),
            P("wide", "dp"),
            P(),
            P("dp", None),
            P("dp", None),
            P("dp", None),
        ),
        out_specs=(
            P(None, "dp", "wide"),
            P(None, "dp", "wide"),
            P("dp", "wide"),
            P("dp", "wide"),
            P("dp", "wide"),
            P("wide", "dp"),
            P("dp", "wide"),
            P("dp", "wide"),
            P("wide", "dp"),
            P(),
            P("wide"),
            P("dp", "wide"),
            P("dp", "wide"),
        ),
        check_vma=False,
    )
```

profile of v0, /device:TPU:0, one launch (start us, length us, event | category | flops | bytes accessed | tf_op | source)
XLA Modules:
  0.0 1579.7 jit_solution(8456090871075567823)
XLA Ops:
  8.9 2.8 multiply_reduce_fusion.15
  11.9 23.4 %all-reduce.3 = (f32[1024]{0:T(1024)S(1)}, f32[1024]{0:T(1024)S(1)}) all-reduce(f32[1024]{0:T(1024)S(1)} %multiply_reduce_fusion.20, f32[1024]{0:T(1024)S(1)} %get-tuple-element.312), channel_id=1, replica_groups=mesh['dp'=4,'wide'=8] {'wide'}, use_global_device_ids=true, to_apply=%region_5.6 | all-reduce | flops 2048 | bytes 16384 | tf_op jit(solution)/shard_map/psum | solution.py:151
  39.9 1.9 fusion.52
  42.8 66.4 %all-gather.12.cloned.1.call-done = bf16[1024,2048]{1,0:T(8,128)(2,1)} async-done(((bf16[1024,256]{1,0:T(8,128)(2,1)}), bf16[1024,2048]{1,0:T(8,128)(2,1)}) %all-gather.12.cloned.1.call-update) | async-done | bytes 4194320 | tf_op jit(solution)/shard_map/all_gather | solution.py:155
  109.2 3.8 fusion.60
  114.0 11.6 all-gather.14.cloned.1.call-done
  125.7 3.9 fusion.59
  134.0 9.8 all-gather.18.cloned.1.call-done
  143.8 3.8 convolution_convert_fusion.1
  147.9 14.2 while.53
  162.7 5.9 fusion.46
  169.5 6.0 multiply_reduce_fusion.6
  175.5 141.2 %reduce-scatter.12.cloned.1.call-done = f32[1024,256]{1,0:T(8,128)} async-done(((f32[1024,2048]{1,0:T(8,128)}), f32[1024,256]{1,0:T(8,128)}) %reduce-scatter.12.cloned.1.call-update) | async-done | bytes 1048592 | tf_op jit(solution)/shard_map/reduce_scatter | solution.py:159
  316.7 5.3 multiply_reduce_fusion.13
  322.2 19.7 %all-reduce.2 = (f32[1024]{0:T(1024)S(1)}, f32[1024]{0:T(1024)S(1)}) all-reduce(f32[1024]{0:T(1024)S(1)} %multiply_reduce_fusion.19, f32[1024]{0:T(1024)S(1)} %get-tuple-element.310), channel_id=1, replica_groups=mesh['dp'=4,'wide'=8] {'wide'}, use_global_device_ids=true, to_apply=%region_18.19 | all-reduce | flops 2048 | bytes 16384 | tf_op jit(solution)/shard_map/psum | solution.py:151
  344.7 7.2 all-gather.24.cloned.1.call-done
  351.8 77.3 %all-gather.22.cloned.1.call-done = bf16[1024,2048]{1,0:T(8,128)(2,1)} async-done(((bf16[1024,256]{1,0:T(8,128)(2,1)}), bf16[1024,2048]{1,0:T(8,128)(2,1)}) %all-gather.22.cloned.1.call-update) | async-done | bytes 4194320 | tf_op jit(solution)/shard_map/all_gather | solution.py:155
  429.1 10.0 fusion.61
  439.1 24.3 %all-gather.26.cloned.1.call-done = bf16[2048,1024]{1,0:T(8,128)(2,1)} async-done(((bf16[512,1024]{1,0:T(8,128)(2,1)}), bf16[2048,1024]{1,0:T(8,128)(2,1)}) %all-gather.26.cloned.1.call-update) | async-done | bytes 4194320 | tf_op jit(solution)/shard_map/all_gather | solution.py:215
  463.3 12.1 multiply_convert_fusion.3
  475.4 23.8 %all-gather.28.cloned.1.call-done = bf16[1024,2048]{1,0:T(8,128)(2,1)} async-done(((bf16[1024,512]{1,0:T(8,128)(2,1)}), bf16[1024,2048]{1,0:T(8,128)(2,1)}) %all-gather.28.cloned.1.call-update) | async-done | bytes 4194320 | tf_op jit(solution)/shard_map/all_gather | solution.py:216
  499.2 10.5 fusion.62
  509.9 10.8 multiply_reduce_fusion.1
  520.7 137.2 %reduce-scatter.14.cloned.1.call-done = f32[1024,256]{1,0:T(8,128)} async-done(((f32[1024,2048]{1,0:T(8,128)}), f32[1024,256]{1,0:T(8,128)}) %reduce-scatter.14.cloned.1.call-update) | async-done | bytes 1048592 | tf_op jit(solution)/shard_map/reduce_scatter | solution.py:159
  657.8 8.0 multiply_reduce_fusion.7
  666.3 73.4 %all-gather.30.cloned.1.call-done = bf16[1024,2048]{1,0:T(8,128)(2,1)} async-done(((bf16[1024,256]{1,0:T(8,128)(2,1)}), bf16[1024,2048]{1,0:T(8,128)(2,1)}) %all-gather.30.cloned.1.call-update) | async-done | bytes 4194320 | tf_op jit(solution)/shard_map/all_gather | solution.py:155
  739.7 12.9 multiply_convert_fusion.1
  752.6 7.0 fusion.63
  759.6 6.9 convolution_add_fusion
  766.6 146.1 %reduce-scatter.16.cloned.1.call-done = f32[1024,256]{1,0:T(8,128)} async-done(((f32[1024,2048]{1,0:T(8,128)}), f32[1024,256]{1,0:T(8,128)}) %reduce-scatter.16.cloned.1.call-update) | async-done | bytes 1048592 | tf_op jit(solution)/shard_map/reduce_scatter | solution.py:175
  914.6 19.9 %all-reduce.1 = (f32[1024]{0:T(1024)S(1)}, f32[1024]{0:T(1024)S(1)}) all-reduce(f32[1024]{0:T(1024)S(1)} %get-tuple-element.326, f32[1024]{0:T(1024)S(1)} %get-tuple-element.325), channel_id=1, replica_groups=mesh['dp'=4,'wide'=8] {'wide'}, use_global_device_ids=true, to_apply=%region_26.27 | all-reduce | flops 2048 | bytes 16384 | tf_op jit(solution)/shard_map/psum | solution.py:151
  936.5 8.4 multiply_reduce_fusion.9
  946.1 2.5 copy.81
  948.7 68.3 %all-gather.32.cloned.1.call-done = bf16[1024,2048]{1,0:T(8,128)(2,1)} async-done(((bf16[1024,256]{1,0:T(8,128)(2,1)}), bf16[1024,2048]{1,0:T(8,128)(2,1)}) %all-gather.32.cloned.1.call-update) | async-done | bytes 4194320 | tf_op jit(solution)/shard_map/all_gather | solution.py:155
  1016.9 3.8 convolution_convert_fusion
  1020.7 30.5 %while.54 = (s32[]{:T(128)}, f32[1024,2,128]{0,2,1:T(8,128)S(1)}, f32[1024,2,128]{0,2,1:T(8,128)}, f32[2,512,2,128]{3,1,2,0:T(8,128)}, s32[2]{0:T(128)S(1)}, /*i...) while((s32[]{:T(128)}, f32[1024,2,128]{0,2,1:T(8,128)S(1)}, ...), condition=%wide.region_31.32_spmd.clone.clone, body=%wide.region_29.31_spmd.clone.sunk.clone | while | flops 1357250560 | bytes 90224648 | solution.py:144
  1024.2 2.2 multiply_reduce_fusion.23
  1030.6 2.6 fusion.178
  1033.2 2.6 fusion.177
  1039.3 2.2 multiply_reduce_fusion.23
  1045.7 2.6 fusion.178
  1048.2 3.0 fusion.177
  1052.6 2.0 copy.71
  1061.2 4.5 add_add_fusion
  1066.0 10.6 fusion.71
  1076.7 10.7 fusion.69
  1087.9 10.7 fusion.70
  1098.7 4.8 fusion.67
  1103.6 5.0 fusion.66
  1108.7 5.1 fusion.44
  1113.9 4.9 fusion.68
  1118.9 6.5 pmax.7
  1126.9 9.0 multiply_reduce_fusion.2
  1135.9 76.0 %reduce-scatter.18.cloned.1.call-done = f32[1024,256]{1,0:T(8,128)} async-done(((f32[1024,2048]{1,0:T(8,128)}), f32[1024,256]{1,0:T(8,128)}) %reduce-scatter.18.cloned.1.call-update) | async-done | bytes 1048592 | tf_op jit(solution)/shard_map/reduce_scatter | solution.py:175
  1213.8 19.7 %all-reduce = (f32[1024]{0:T(1024)S(1)}, f32[1024]{0:T(1024)S(1)}) all-reduce(f32[1024]{0:T(1024)S(1)} %get-tuple-element.324, f32[1024]{0:T(1024)S(1)} %get-tuple-element.323), channel_id=1, replica_groups=mesh['dp'=4,'wide'=8] {'wide'}, use_global_device_ids=true, to_apply=%region_36.37 | all-reduce | flops 2048 | bytes 16384 | tf_op jit(solution)/shard_map/psum | solution.py:151
  1235.4 7.2 multiply_reduce_fusion.10
  1242.9 38.0 %psum.71 = f32[2,4,6]{2,1,0:T(4,128)} all-reduce(f32[2,4,6]{2,1,0:T(4,128)S(1)} %pad_maximum_fusion.3), channel_id=1, replica_groups=mesh['dp'=4,'wide'=8] {'dp','wide'}, use_global_device_ids=true, to_apply=%region_50.51 | all-reduce | flops 48 | bytes 384 | tf_op jit(solution)/shard_map/psum | solution.py:330
  1280.9 5.8 reduce-scatter.32.cloned.1.call-done
  1286.7 74.4 %reduce-scatter.28.cloned.1.call-done = f32[512,1024]{1,0:T(8,128)} async-done(((f32[2048,1024]{1,0:T(8,128)}), f32[512,1024]{1,0:T(8,128)}) %reduce-scatter.28.cloned.1.call-update) | async-done | bytes 2097168 | tf_op jit(solution)/shard_map/reduce_scatter | solution.py:264
  1361.1 74.4 %reduce-scatter.30.cloned.1.call-done = f32[512,1024]{1,0:T(8,128)} async-done(((f32[2048,1024]{1,0:T(8,128)}), f32[512,1024]{1,0:T(8,128)}) %reduce-scatter.30.cloned.1.call-update) | async-done | bytes 2097168 | tf_op jit(solution)/shard_map/reduce_scatter | solution.py:265
  1435.6 34.3 %reduce-scatter.22.cloned.1.call-done = f32[512,256]{1,0:T(8,128)} async-done(((f32[2048,256]{1,0:T(8,128)}), f32[512,256]{1,0:T(8,128)}) %reduce-scatter.22.cloned.1.call-update) | async-done | bytes 524304 | tf_op jit(solution)/shard_map/reduce_scatter | solution.py:341
  1469.9 34.2 %reduce-scatter.20.cloned.1.call-done = f32[512,256]{1,0:T(8,128)} async-done(((f32[2048,256]{1,0:T(8,128)}), f32[512,256]{1,0:T(8,128)}) %reduce-scatter.20.cloned.1.call-update) | async-done | bytes 524304 | tf_op jit(solution)/shard_map/reduce_scatter | solution.py:340
  1504.0 34.3 %reduce-scatter.26.cloned.1.call-done = f32[256,512]{1,0:T(8,128)} async-done(((f32[256,2048]{1,0:T(8,128)}), f32[256,512]{1,0:T(8,128)}) %reduce-scatter.26.cloned.1.call-update) | async-done | bytes 524304 | tf_op jit(solution)/shard_map/reduce_scatter | solution.py:343
  1538.4 34.3 %reduce-scatter.24.cloned.1.call-done = f32[512,256]{1,0:T(8,128)} async-done(((f32[2048,256]{1,0:T(8,128)}), f32[512,256]{1,0:T(8,128)}) %reduce-scatter.24.cloned.1.call-update) | async-done | bytes 524304 | tf_op jit(solution)/shard_map/reduce_scatter | solution.py:342
  (262 shorter events, 63.1 us)
Async XLA Ops:
  7.2 35.6 %all-gather.16.cloned.1.call-start = ((), (), s32[]{:S(2)}) async-start(), calls=%async_computation.13 | async-start | bytes 1310720 | tf_op jit(solution)/shard_map/all_gather | solution.py:209
  7.9 101.3 %all-gather.12.cloned.1.call-start = ((), (), s32[]{:S(2)}) async-start(), calls=%async_computation.11 | async-start | bytes 4718592 | tf_op jit(solution)/shard_map/all_gather | solution.py:155
  11.7 30.7 %copy-start.2 = (f32[1024,256]{1,0:T(8,128)}, f32[1024,256]{1,0:T(8,128)S(1)}, u32[]{:S(2)}) copy-start(f32[1024,256]{1,0:T(8,128)S(1)} %get-tuple-element.313) | copy-start | bytes 3145732
  36.0 6.7 copy-start.43
  36.0 6.7 copy-start.46
  37.1 88.5 %all-gather.14.cloned.1.call-start = ((), (), s32[]{:S(2)}) async-start(), calls=%async_computation.12 | async-start | bytes 1310720 | tf_op jit(solution)/shard_map/all_gather | solution.py:208
  37.9 105.9 %all-gather.18.cloned.1.call-start = ((), (), s32[]{:S(2)}) async-start(), calls=%async_computation.14 | async-start | bytes 1310720 | tf_op jit(solution)/shard_map/all_gather | solution.py:210
  38.5 124.3 %all-gather.20.cloned.1.call-start = ((), (), s32[]{:S(2)}) async-start(), calls=%async_computation.15 | async-start | bytes 1310720 | tf_op jit(solution)/shard_map/all_gather | solution.py:211
  39.0 277.6 %reduce-scatter.12.cloned.1.call-start = ((), (), s32[]{:S(2)}) async-start(), calls=%async_computation.16 | async-start | bytes 9437184 | tf_op jit(solution)/shard_map/reduce_scatter | solution.py:159
  42.2 70.7 %copy-start.16 = (f32[1024,128]{1,0:T(8,128)}, f32[1024,128]{1,0:T(8,128)S(1)}, u32[]{:S(2)}) copy-start(f32[1024,128]{1,0:T(8,128)S(1)} %get-tuple-element.422) | copy-start | bytes 1572868
  42.5 902.6 %copy-start.12 = (f32[1024,128]{0,1:T(8,128)}, f32[1024,128]{0,1:T(8,128)S(1)}, u32[]{:S(2)}) copy-start(f32[1024,128]{0,1:T(8,128)S(1)} %copy.61) | copy-start | bytes 1572868
  42.7 87.0 %copy-start.14 = (f32[1024,128]{0,1:T(8,128)}, f32[1024,128]{0,1:T(8,128)S(1)}, u32[]{:S(2)}) copy-start(f32[1024,128]{0,1:T(8,128)S(1)} %copy.62) | copy-start | bytes 1572868
  125.7 4.0 copy-start.22
  125.7 4.0 copy-start.23
  133.9 13.9 copy-start.21
  134.0 13.9 copy-start.29
  162.1 6.5 copy-start.41
  162.7 5.9 copy-start.19
  168.6 183.2 %all-gather.24.cloned.1.call-start = ((), (), s32[]{:S(2)}) async-start(), calls=%async_computation.18 | async-start | bytes 5242880 | tf_op jit(solution)/shard_map/all_gather | solution.py:214
  169.4 259.7 %all-gather.22.cloned.1.call-start = ((), (), s32[]{:S(2)}) async-start(), calls=%async_computation.17 | async-start | bytes 4718592 | tf_op jit(solution)/shard_map/all_gather | solution.py:155
  169.5 6.0 copy-start.35
  343.1 120.2 %all-gather.26.cloned.1.call-start = ((), (), s32[]{:S(2)}) async-start(), calls=%async_computation.19 | async-start | bytes 5242880 | tf_op jit(solution)/shard_map/all_gather | solution.py:215
  343.8 155.4 %all-gather.28.cloned.1.call-start = ((), (), s32[]{:S(2)}) async-start(), calls=%async_computation.20 | async-start | bytes 5242880 | tf_op jit(solution)/shard_map/all_gather | solution.py:216
  344.4 313.4 %reduce-scatter.14.cloned.1.call-start = ((), (), s32[]{:S(2)}) async-start(), calls=%async_computation.21 | async-start | bytes 9437184 | tf_op jit(solution)/shard_map/reduce_scatter | solution.py:159
  509.8 229.9 %all-gather.30.cloned.1.call-start = ((), (), s32[]{:S(2)}) async-start(), calls=%async_computation.22 | async-start | bytes 4718592 | tf_op jit(solution)/shard_map/all_gather | solution.py:155
  665.9 246.9 %reduce-scatter.16.cloned.1.call-start = ((), (), s32[]{:S(2)}) async-start(), calls=%async_computation.23 | async-start | bytes 9437184 | tf_op jit(solution)/shard_map/reduce_scatter | solution.py:175
  739.7 12.9 copy-start.44
  752.6 7.0 copy-start.48
  752.6 7.0 copy-start.45
  766.6 250.4 %all-gather.32.cloned.1.call-start = ((), (), s32[]{:S(2)}) async-start(), calls=%async_computation.24 | async-start | bytes 4718592 | tf_op jit(solution)/shard_map/all_gather | solution.py:155
  944.9 267.0 %reduce-scatter.18.cloned.1.call-start = ((), (), s32[]{:S(2)}) async-start(), calls=%async_computation.25 | async-start | bytes 9437184 | tf_op jit(solution)/shard_map/reduce_scatter | solution.py:175
  1020.7 5.7 copy-start.4
  1020.7 5.7 copy-start.8
  1020.8 5.7 copy-start.10
  1020.8 5.7 copy-start.6
  1028.8 4.4 copy-start.1
  1035.8 5.7 copy-start.4
  1035.8 5.7 copy-start.8
  1035.8 5.7 copy-start.10
  1035.8 5.7 copy-start.6
  1043.9 4.4 copy-start.1
  1048.2 3.0 copy-start.9
  1048.2 3.0 copy-start.11
  1051.2 3.4 copy-start.15
  1051.2 3.7 copy-start.17
  1065.7 221.0 %reduce-scatter.32.cloned.1.call-start = ((), (), s32[]{:S(2)}) async-start(), calls=%async_computation.32 | async-start | bytes 10485760 | tf_op jit(solution)/shard_map/reduce_scatter | solution.py:266
  1076.6 284.5 %reduce-scatter.28.cloned.1.call-start = ((), (), s32[]{:S(2)}) async-start(), calls=%async_computation.30 | async-start | bytes 10485760 | tf_op jit(solution)/shard_map/reduce_scatter | solution.py:264
  1087.4 348.2 %reduce-scatter.30.cloned.1.call-start = ((), (), s32[]{:S(2)}) async-start(), calls=%async_computation.31 | async-start | bytes 10485760 | tf_op jit(solution)/shard_map/reduce_scatter | solution.py:265
  1098.6 371.3 %reduce-scatter.22.cloned.1.call-start = ((), (), s32[]{:S(2)}) async-start(), calls=%async_computation.27 | async-start | bytes 2621440 | tf_op jit(solution)/shard_map/reduce_scatter | solution.py:341
  1103.5 5.2 copy-start.20
  1103.5 400.5 %reduce-scatter.20.cloned.1.call-start = ((), (), s32[]{:S(2)}) async-start(), calls=%async_computation.26 | async-start | bytes 2621440 | tf_op jit(solution)/shard_map/reduce_scatter | solution.py:340
  1108.6 429.7 %reduce-scatter.26.cloned.1.call-start = ((), (), s32[]{:S(2)}) async-start(), calls=%async_computation.29 | async-start | bytes 2621440 | tf_op jit(solution)/shard_map/reduce_scatter | solution.py:343
  1113.8 5.1 copy-start.42
  1113.8 11.6 copy-start.27
  1113.8 11.6 copy-start.28
  1113.8 12.7 copy-start.40
  1113.8 13.0 copy-start.37
  1113.9 13.0 copy-start.36
  1113.9 458.8 %reduce-scatter.24.cloned.1.call-start = ((), (), s32[]{:S(2)}) async-start(), calls=%async_computation.28 | async-start | bytes 2621440 | tf_op jit(solution)/shard_map/reduce_scatter | solution.py:342
  1125.4 10.5 copy-start.47
  1126.9 85.0 %copy-start.3 = (f32[1024,256]{1,0:T(8,128)S(1)}, f32[1024,256]{1,0:T(8,128)}, u32[]{:S(2)}) copy-start(f32[1024,256]{1,0:T(8,128)} %copy-done.2) | copy-start | bytes 3145732
  1126.9 85.0 %copy-start.31 = (f32[1024]{0:T(1024)S(1)}, f32[1024]{0:T(1024)}, u32[]{:S(2)}) copy-start(f32[1024]{0:T(1024)} %copy-done.30) | copy-start | bytes 12292
  1126.9 85.0 %copy-start.33 = (f32[1024]{0:T(1024)S(1)}, f32[1024]{0:T(1024)}, u32[]{:S(2)}) copy-start(f32[1024]{0:T(1024)} %copy-done.32) | copy-start | bytes 12292
  1135.9 99.5 %copy-start.39 = (f32[4]{0:T(128)S(1)}, f32[4]{0:T(128)}, u32[]{:S(2)}) copy-start(f32[4]{0:T(128)} %copy-done.38) | copy-start | bytes 52
  (17 other events, 34.8 us)
Sparse Core Ops, SparseCore 0:
  9.5 19.4 all-gather.15
  37.3 71.8 all-gather.11
  110.8 14.8 all-gather.13
  127.1 16.6 all-gather.17
  145.2 16.6 all-gather.19
  168.7 147.8 reduce-scatter.11
  318.2 33.5 all-gather.23
  354.4 74.6 all-gather.21
  430.7 32.6 all-gather.25
  464.7 34.4 all-gather.27
  509.9 147.8 reduce-scatter.13
  666.0 73.7 all-gather.29
  766.7 146.0 reduce-scatter.15
  945.1 71.8 all-gather.31
  1065.9 146.0 reduce-scatter.17
  1214.9 71.7 reduce-scatter.31
  1289.7 71.3 reduce-scatter.27
  1364.1 71.3 reduce-scatter.29
  1438.7 31.1 reduce-scatter.21
  1472.8 31.1 reduce-scatter.19
  1507.2 31.1 reduce-scatter.25
  1541.5 31.1 reduce-scatter.23
where the time goes:
time: 1590 us; the launch traced here: 1580 us
  waiting for transfers between devices  1160 us (73%)
  matrix products  165 us (10%)
  blocking collectives  127 us (8%)
  other arithmetic  86.2 us (5%)
  local copies, waits for them, and re-layouts  21 us (1%)
    all_gather x4, waiting for transfers between devices, features(): return lax.all_gather(piece, 'wide', axis=1, tiled=True)  285 us
    reduce_scatter x2, waiting for transfers between devices, branch_rows(): lax.psum_scatter(partial_value, 'wide', scatter_dimension=1, tiled=True)  278 us
    reduce_scatter x2, waiting for transfers between devices, norm_backward(): lax.psum_scatter(partial_value, 'wide', scatter_dimension=1, tiled=True)  222 us
    psum x4, blocking collectives, row_sums(): lax.psum((jnp.sum(first_term, axis=1), jnp.sum(second_term, axis=1)), 'wi...  82.8 us
    reduce_scatter x1, waiting for transfers between devices, per_device(): lax.psum_scatter(up_wgrad, 'dp', scatter_dimension=0, tiled=True)  74.4 us
    reduce_scatter x1, waiting for transfers between devices, per_device(): lax.psum_scatter(gate_wgrad, 'dp', scatter_dimension=0, tiled=True)  74.4 us
    psum x1, blocking collectives, per_device(): lax.psum(jnp.stack([hyper_rows(attn_pre_grad, attn_post_grad, attn_mix_gr...  38 us
    reduce_scatter x1, waiting for transfers between devices, per_device(): lax.psum_scatter(out_wgrad, 'dp', scatter_dimension=1, tiled=True)  34.3 us
  transfers between devices with their start and end apart: 22, of which 20 were waited for; matrix products, arithmetic and copies ran while one was open for 10% of the time, Pallas kernels for 0%

commit v1 on v0

--- a/solution.py
+++ b/solution.py
@@ -327,7 +327,7 @@
     h_one_grad = norm_backward(normed_one_grad, kept_one, inverse_one)
     attn_pre_grad = jnp.sum(h_one_grad[None, :, :] * streams, axis=(1, 2))
     streams_grad = mix_back(attn_mix, after_grad) + attn_pre[:, None, None] * h_one_grad[None, :, :]
-    hyper_grad = lax.psum(
+    hyper_grad = jax.lax.all_gather(
         jnp.stack(
             [
                 hyper_rows(attn_pre_grad, attn_post_grad, attn_mix_grad),
@@ -335,7 +335,7 @@
             ]
         ),
         ("dp", "wide"),
-    )
+    ).sum(axis=0)
     query_shard, key_shard, value_shard, out_shard = (
         lax.psum_scatter(query_wgrad, "dp", scatter_dimension=0, tiled=True),
         lax.psum_scatter(key_wgrad, "dp", scatter_dimension=0, tiled=True),

time: 1590 us -> 1590 us (level)
  waiting for transfers between devices: 1160 us -> 1130 us
  blocking collectives: 127 us -> 154 us
    all_gather x0 -> x1, blocking collectives: none -> 65 us  [per_device(): jax.lax.all_gather(jnp.stack([hyper_rows(attn_pre_grad, attn_post_grad, a...]
    psum x1 -> x0, blocking collectives: 38 us -> none  [per_device(): lax.psum(jnp.stack([hyper_rows(attn_pre_grad, attn_post_grad, attn_mix_gr...]
    reduce_scatter x1, waiting for transfers between devices: 74.4 us -> 51.2 us  [per_device(): lax.psum_scatter(gate_wgrad, 'dp', scatter_dimension=0, tiled=True)]
  transfers between devices with their start and end apart: 22 -> 22, of which waited for: 20 -> 19; matrix products, arithmetic and copies ran while one was open for 10% -> 10% of each run, Pallas kernels for 0% -> 0%
where the time goes in v1:
time: 1590 us; the launch traced here: 1580 us
  waiting for transfers between devices  1130 us (71%)
  matrix products  165 us (10%)
  blocking collectives  154 us (10%)
  other arithmetic  86.8 us (5%)
  local copies, waits for them, and re-layouts  21 us (1%)
    all_gather x4, waiting for transfers between devices, features(): return lax.all_gather(piece, 'wide', axis=1, tiled=True)  285 us
    reduce_scatter x2, waiting for transfers between devices, branch_rows(): lax.psum_scatter(partial_value, 'wide', scatter_dimension=1, tiled=True)  278 us
    reduce_scatter x2, waiting for transfers between devices, norm_backward(): lax.psum_scatter(partial_value, 'wide', scatter_dimension=1, tiled=True)  222 us
    psum x4, blocking collectives, row_sums(): lax.psum((jnp.sum(first_term, axis=1), jnp.sum(second_term, axis=1)), 'wi...  82.8 us
    reduce_scatter x1, waiting for transfers between devices, per_device(): lax.psum_scatter(up_wgrad, 'dp', scatter_dimension=0, tiled=True)  74.4 us
    all_gather x1, blocking collectives, per_device(): jax.lax.all_gather(jnp.stack([hyper_rows(attn_pre_grad, attn_post_grad, a...  65 us
    reduce_scatter x1, waiting for transfers between devices, per_device(): lax.psum_scatter(gate_wgrad, 'dp', scatter_dimension=0, tiled=True)  51.2 us
    reduce_scatter x1, waiting for transfers between devices, per_device(): lax.psum_scatter(out_wgrad, 'dp', scatter_dimension=1, tiled=True)  34.3 us
  transfers between devices with their start and end apart: 22, of which 19 were waited for; matrix products, arithmetic and copies ran while one was open for 10% of the time, Pallas kernels for 0%

profile of v1, /device:TPU:0, one launch (start us, length us, event | category | flops | bytes accessed | tf_op | source)
XLA Modules:
  0.0 1578.3 jit_solution(4935239182831670344)
XLA Ops:
  8.9 2.8 multiply_reduce_fusion.15
  11.9 23.4 %all-reduce.3 = (f32[1024]{0:T(1024)S(1)}, f32[1024]{0:T(1024)S(1)}) all-reduce(f32[1024]{0:T(1024)S(1)} %multiply_reduce_fusion.20, f32[1024]{0:T(1024)S(1)} %get-tuple-element.334), channel_id=1, replica_groups=mesh['dp'=4,'wide'=8] {'wide'}, use_global_device_ids=true, to_apply=%region_5.6 | all-reduce | flops 2048 | bytes 16384 | tf_op jit(solution)/shard_map/psum | solution.py:151
  39.9 1.9 fusion.52
  42.8 66.4 %all-gather.13.cloned.1.call-done = bf16[1024,2048]{1,0:T(8,128)(2,1)} async-done(((bf16[1024,256]{1,0:T(8,128)(2,1)}), bf16[1024,2048]{1,0:T(8,128)(2,1)}) %all-gather.13.cloned.1.call-update) | async-done | bytes 4194320 | tf_op jit(solution)/shard_map/all_gather | solution.py:155
  109.2 3.8 fusion.60
  114.0 11.6 all-gather.15.cloned.1.call-done
  125.7 3.9 fusion.59
  134.0 9.8 all-gather.19.cloned.1.call-done
  143.8 3.8 convolution_convert_fusion.1
  147.9 14.2 while.53
  162.7 5.9 fusion.46
  169.5 6.0 multiply_reduce_fusion.6
  175.5 141.2 %reduce-scatter.12.cloned.1.call-done = f32[1024,256]{1,0:T(8,128)} async-done(((f32[1024,2048]{1,0:T(8,128)}), f32[1024,256]{1,0:T(8,128)}) %reduce-scatter.12.cloned.1.call-update) | async-done | bytes 1048592 | tf_op jit(solution)/shard_map/reduce_scatter | solution.py:159
  316.7 5.3 multiply_reduce_fusion.13
  322.2 19.7 %all-reduce.2 = (f32[1024]{0:T(1024)S(1)}, f32[1024]{0:T(1024)S(1)}) all-reduce(f32[1024]{0:T(1024)S(1)} %multiply_reduce_fusion.19, f32[1024]{0:T(1024)S(1)} %get-tuple-element.332), channel_id=1, replica_groups=mesh['dp'=4,'wide'=8] {'wide'}, use_global_device_ids=true, to_apply=%region_18.19 | all-reduce | flops 2048 | bytes 16384 | tf_op jit(solution)/shard_map/psum | solution.py:151
  344.7 7.2 all-gather.25.cloned.1.call-done
  351.8 77.3 %all-gather.23.cloned.1.call-done = bf16[1024,2048]{1,0:T(8,128)(2,1)} async-done(((bf16[1024,256]{1,0:T(8,128)(2,1)}), bf16[1024,2048]{1,0:T(8,128)(2,1)}) %all-gather.23.cloned.1.call-update) | async-done | bytes 4194320 | tf_op jit(solution)/shard_map/all_gather | solution.py:155
  429.1 10.0 fusion.61
  439.1 24.3 %all-gather.27.cloned.1.call-done = bf16[2048,1024]{1,0:T(8,128)(2,1)} async-done(((bf16[512,1024]{1,0:T(8,128)(2,1)}), bf16[2048,1024]{1,0:T(8,128)(2,1)}) %all-gather.27.cloned.1.call-update) | async-done | bytes 4194320 | tf_op jit(solution)/shard_map/all_gather | solution.py:215
  463.3 12.1 multiply_convert_fusion.3
  475.4 23.8 %all-gather.29.cloned.1.call-done = bf16[1024,2048]{1,0:T(8,128)(2,1)} async-done(((bf16[1024,512]{1,0:T(8,128)(2,1)}), bf16[1024,2048]{1,0:T(8,128)(2,1)}) %all-gather.29.cloned.1.call-update) | async-done | bytes 4194320 | tf_op jit(solution)/shard_map/all_gather | solution.py:216
  499.2 10.5 fusion.62
  509.9 10.8 multiply_reduce_fusion.1
  520.7 137.2 %reduce-scatter.14.cloned.1.call-done = f32[1024,256]{1,0:T(8,128)} async-done(((f32[1024,2048]{1,0:T(8,128)}), f32[1024,256]{1,0:T(8,128)}) %reduce-scatter.14.cloned.1.call-update) | async-done | bytes 1048592 | tf_op jit(solution)/shard_map/reduce_scatter | solution.py:159
  657.8 8.0 multiply_reduce_fusion.7
  666.3 73.4 %all-gather.31.cloned.1.call-done = bf16[1024,2048]{1,0:T(8,128)(2,1)} async-done(((bf16[1024,256]{1,0:T(8,128)(2,1)}), bf16[1024,2048]{1,0:T(8,128)(2,1)}) %all-gather.31.cloned.1.call-update) | async-done | bytes 4194320 | tf_op jit(solution)/shard_map/all_gather | solution.py:155
  739.7 12.9 multiply_convert_fusion.1
  752.6 7.0 fusion.63
  759.6 6.9 convolution_add_fusion
  766.6 146.1 %reduce-scatter.16.cloned.1.call-done = f32[1024,256]{1,0:T(8,128)} async-done(((f32[1024,2048]{1,0:T(8,128)}), f32[1024,256]{1,0:T(8,128)}) %reduce-scatter.16.cloned.1.call-update) | async-done | bytes 1048592 | tf_op jit(solution)/shard_map/reduce_scatter | solution.py:175
  914.6 19.9 %all-reduce.1 = (f32[1024]{0:T(1024)S(1)}, f32[1024]{0:T(1024)S(1)}) all-reduce(f32[1024]{0:T(1024)S(1)} %get-tuple-element.348, f32[1024]{0:T(1024)S(1)} %get-tuple-element.347), channel_id=1, replica_groups=mesh['dp'=4,'wide'=8] {'wide'}, use_global_device_ids=true, to_apply=%region_26.27 | all-reduce | flops 2048 | bytes 16384 | tf_op jit(solution)/shard_map/psum | solution.py:151
  934.6 1.9 subtract_multiply_fusion.1
  936.5 8.4 multiply_reduce_fusion.9
  946.1 2.5 copy.101
  948.7 68.3 %all-gather.33.cloned.1.call-done = bf16[1024,2048]{1,0:T(8,128)(2,1)} async-done(((bf16[1024,256]{1,0:T(8,128)(2,1)}), bf16[1024,2048]{1,0:T(8,128)(2,1)}) %all-gather.33.cloned.1.call-update) | async-done | bytes 4194320 | tf_op jit(solution)/shard_map/all_gather | solution.py:155
  1016.9 3.8 convolution_convert_fusion
  1020.7 30.5 %while.54 = (s32[]{:T(128)}, f32[1024,2,128]{0,2,1:T(8,128)S(1)}, f32[1024,2,128]{0,2,1:T(8,128)}, f32[2,512,2,128]{3,1,2,0:T(8,128)}, s32[2]{0:T(128)S(1)}, /*i...) while((s32[]{:T(128)}, f32[1024,2,128]{0,2,1:T(8,128)S(1)}, ...), condition=%wide.region_31.32_spmd.clone.clone, body=%wide.region_29.31_spmd.clone.sunk.clone | while | flops 1357250560 | bytes 90224648 | solution.py:144
  1024.2 2.2 multiply_reduce_fusion.23
  1030.6 2.6 fusion.178
  1033.2 2.6 fusion.177
  1039.3 2.2 multiply_reduce_fusion.23
  1045.7 2.6 fusion.178
  1048.2 3.0 fusion.177
  1052.6 2.0 copy.91
  1061.2 4.5 add_add_fusion
  1066.0 10.6 fusion.71
  1076.7 10.7 fusion.69
  1087.9 10.7 fusion.70
  1098.7 4.8 fusion.67
  1103.6 5.0 fusion.66
  1108.7 5.1 fusion.44
  1113.9 4.9 fusion.68
  1118.9 6.5 pmax.7
  1126.9 9.0 multiply_reduce_fusion.2
  1135.9 76.0 %reduce-scatter.18.cloned.1.call-done = f32[1024,256]{1,0:T(8,128)} async-done(((f32[1024,2048]{1,0:T(8,128)}), f32[1024,256]{1,0:T(8,128)}) %reduce-scatter.18.cloned.1.call-update) | async-done | bytes 1048592 | tf_op jit(solution)/shard_map/reduce_scatter | solution.py:175
  1213.8 19.7 %all-reduce = (f32[1024]{0:T(1024)S(1)}, f32[1024]{0:T(1024)S(1)}) all-reduce(f32[1024]{0:T(1024)S(1)} %get-tuple-element.346, f32[1024]{0:T(1024)S(1)} %get-tuple-element.345), channel_id=1, replica_groups=mesh['dp'=4,'wide'=8] {'wide'}, use_global_device_ids=true, to_apply=%region_36.37 | all-reduce | flops 2048 | bytes 16384 | tf_op jit(solution)/shard_map/psum | solution.py:151
  1235.4 7.2 multiply_reduce_fusion.10
  1242.9 65.0 %all-gather = f32[64,4,6]{2,1,0:T(4,128)S(1)} all-gather(f32[2,4,6]{2,1,0:T(4,128)S(1)} %pad_maximum_fusion.3), channel_id=2, replica_groups=mesh['dp'=4,'wide'=8] {'dp','wide'}, dimensions={0}, use_global_device_ids=true | all-gather | bytes 6336 | tf_op jit(solution)/shard_map/all_gather | solution.py:330
  1308.5 51.2 %reduce-scatter.28.cloned.1.call-done = f32[512,1024]{1,0:T(8,128)} async-done(((f32[2048,1024]{1,0:T(8,128)}), f32[512,1024]{1,0:T(8,128)}) %reduce-scatter.28.cloned.1.call-update) | async-done | bytes 2097168 | tf_op jit(solution)/shard_map/reduce_scatter | solution.py:264
  1359.7 74.4 %reduce-scatter.30.cloned.1.call-done = f32[512,1024]{1,0:T(8,128)} async-done(((f32[2048,1024]{1,0:T(8,128)}), f32[512,1024]{1,0:T(8,128)}) %reduce-scatter.30.cloned.1.call-update) | async-done | bytes 2097168 | tf_op jit(solution)/shard_map/reduce_scatter | solution.py:265
  1434.2 34.3 %reduce-scatter.22.cloned.1.call-done = f32[512,256]{1,0:T(8,128)} async-done(((f32[2048,256]{1,0:T(8,128)}), f32[512,256]{1,0:T(8,128)}) %reduce-scatter.22.cloned.1.call-update) | async-done | bytes 524304 | tf_op jit(solution)/shard_map/reduce_scatter | solution.py:341
  1468.5 34.2 %reduce-scatter.20.cloned.1.call-done = f32[512,256]{1,0:T(8,128)} async-done(((f32[2048,256]{1,0:T(8,128)}), f32[512,256]{1,0:T(8,128)}) %reduce-scatter.20.cloned.1.call-update) | async-done | bytes 524304 | tf_op jit(solution)/shard_map/reduce_scatter | solution.py:340
  1502.6 34.3 %reduce-scatter.26.cloned.1.call-done = f32[256,512]{1,0:T(8,128)} async-done(((f32[256,2048]{1,0:T(8,128)}), f32[256,512]{1,0:T(8,128)}) %reduce-scatter.26.cloned.1.call-update) | async-done | bytes 524304 | tf_op jit(solution)/shard_map/reduce_scatter | solution.py:343
  1537.0 34.3 %reduce-scatter.24.cloned.1.call-done = f32[512,256]{1,0:T(8,128)} async-done(((f32[2048,256]{1,0:T(8,128)}), f32[512,256]{1,0:T(8,128)}) %reduce-scatter.24.cloned.1.call-update) | async-done | bytes 524304 | tf_op jit(solution)/shard_map/reduce_scatter | solution.py:342
  (263 shorter events, 61.9 us)
Async XLA Ops:
  7.2 35.6 %all-gather.17.cloned.1.call-start = ((), (), s32[]{:S(2)}) async-start(), calls=%async_computation.13 | async-start | bytes 1310720 | tf_op jit(solution)/shard_map/all_gather | solution.py:209
  7.9 101.3 %all-gather.13.cloned.1.call-start = ((), (), s32[]{:S(2)}) async-start(), calls=%async_computation.11 | async-start | bytes 4718592 | tf_op jit(solution)/shard_map/all_gather | solution.py:155
  11.7 30.7 %copy-start.2 = (f32[1024,256]{1,0:T(8,128)}, f32[1024,256]{1,0:T(8,128)S(1)}, u32[]{:S(2)}) copy-start(f32[1024,256]{1,0:T(8,128)S(1)} %get-tuple-element.335) | copy-start | bytes 3145732
  36.0 6.7 copy-start.43
  36.0 6.7 copy-start.46
  37.1 88.5 %all-gather.15.cloned.1.call-start = ((), (), s32[]{:S(2)}) async-start(), calls=%async_computation.12 | async-start | bytes 1310720 | tf_op jit(solution)/shard_map/all_gather | solution.py:208
  37.9 105.9 %all-gather.19.cloned.1.call-start = ((), (), s32[]{:S(2)}) async-start(), calls=%async_computation.14 | async-start | bytes 1310720 | tf_op jit(solution)/shard_map/all_gather | solution.py:210
  38.5 124.3 %all-gather.21.cloned.1.call-start = ((), (), s32[]{:S(2)}) async-start(), calls=%async_computation.15 | async-start | bytes 1310720 | tf_op jit(solution)/shard_map/all_gather | solution.py:211
  39.0 277.6 %reduce-scatter.12.cloned.1.call-start = ((), (), s32[]{:S(2)}) async-start(), calls=%async_computation.16 | async-start | bytes 9437184 | tf_op jit(solution)/shard_map/reduce_scatter | solution.py:159
  42.2 70.7 %copy-start.16 = (f32[1024,128]{1,0:T(8,128)}, f32[1024,128]{1,0:T(8,128)S(1)}, u32[]{:S(2)}) copy-start(f32[1024,128]{1,0:T(8,128)S(1)} %get-tuple-element.444) | copy-start | bytes 1572868
  42.5 902.6 %copy-start.12 = (f32[1024,128]{0,1:T(8,128)}, f32[1024,128]{0,1:T(8,128)S(1)}, u32[]{:S(2)}) copy-start(f32[1024,128]{0,1:T(8,128)S(1)} %copy.81) | copy-start | bytes 1572868
  42.7 87.0 %copy-start.14 = (f32[1024,128]{0,1:T(8,128)}, f32[1024,128]{0,1:T(8,128)S(1)}, u32[]{:S(2)}) copy-start(f32[1024,128]{0,1:T(8,128)S(1)} %copy.82) | copy-start | bytes 1572868
  125.7 4.0 copy-start.22
  125.7 4.0 copy-start.23
  133.9 13.9 copy-start.21
  134.0 13.9 copy-start.29
  162.1 6.5 copy-start.41
  162.7 5.9 copy-start.19
  168.6 183.2 %all-gather.25.cloned.1.call-start = ((), (), s32[]{:S(2)}) async-start(), calls=%async_computation.18 | async-start | bytes 5242880 | tf_op jit(solution)/shard_map/all_gather | solution.py:214
  169.4 259.7 %all-gather.23.cloned.1.call-start = ((), (), s32[]{:S(2)}) async-start(), calls=%async_computation.17 | async-start | bytes 4718592 | tf_op jit(solution)/shard_map/all_gather | solution.py:155
  169.5 6.0 copy-start.35
  343.1 120.2 %all-gather.27.cloned.1.call-start = ((), (), s32[]{:S(2)}) async-start(), calls=%async_computation.19 | async-start | bytes 5242880 | tf_op jit(solution)/shard_map/all_gather | solution.py:215
  343.8 155.4 %all-gather.29.cloned.1.call-start = ((), (), s32[]{:S(2)}) async-start(), calls=%async_computation.20 | async-start | bytes 5242880 | tf_op jit(solution)/shard_map/all_gather | solution.py:216
  344.4 313.4 %reduce-scatter.14.cloned.1.call-start = ((), (), s32[]{:S(2)}) async-start(), calls=%async_computation.21 | async-start | bytes 9437184 | tf_op jit(solution)/shard_map/reduce_scatter | solution.py:159
  509.8 229.9 %all-gather.31.cloned.1.call-start = ((), (), s32[]{:S(2)}) async-start(), calls=%async_computation.22 | async-start | bytes 4718592 | tf_op jit(solution)/shard_map/all_gather | solution.py:155
  665.9 246.9 %reduce-scatter.16.cloned.1.call-start = ((), (), s32[]{:S(2)}) async-start(), calls=%async_computation.23 | async-start | bytes 9437184 | tf_op jit(solution)/shard_map/reduce_scatter | solution.py:175
  739.7 12.9 copy-start.44
  752.6 7.0 copy-start.48
  752.6 7.0 copy-start.45
  766.6 250.4 %all-gather.33.cloned.1.call-start = ((), (), s32[]{:S(2)}) async-start(), calls=%async_computation.24 | async-start | bytes 4718592 | tf_op jit(solution)/shard_map/all_gather | solution.py:155
  944.9 267.0 %reduce-scatter.18.cloned.1.call-start = ((), (), s32[]{:S(2)}) async-start(), calls=%async_computation.25 | async-start | bytes 9437184 | tf_op jit(solution)/shard_map/reduce_scatter | solution.py:175
  1020.7 5.7 copy-start.4
  1020.7 5.7 copy-start.8
  1020.8 5.7 copy-start.10
  1020.8 5.7 copy-start.6
  1028.8 4.4 copy-start.1
  1035.8 5.7 copy-start.4
  1035.8 5.7 copy-start.8
  1035.8 5.7 copy-start.10
  1035.8 5.7 copy-start.6
  1043.9 4.4 copy-start.1
  1048.2 3.0 copy-start.9
  1048.2 3.0 copy-start.11
  1051.2 3.4 copy-start.15
  1051.2 3.7 copy-start.17
  1065.7 242.8 %reduce-scatter.32.cloned.1.call-start = ((), (), s32[]{:S(2)}) async-start(), calls=%async_computation.32 | async-start | bytes 10485760 | tf_op jit(solution)/shard_map/reduce_scatter | solution.py:266
  1076.6 283.1 %reduce-scatter.28.cloned.1.call-start = ((), (), s32[]{:S(2)}) async-start(), calls=%async_computation.30 | async-start | bytes 10485760 | tf_op jit(solution)/shard_map/reduce_scatter | solution.py:264
  1087.4 346.8 %reduce-scatter.30.cloned.1.call-start = ((), (), s32[]{:S(2)}) async-start(), calls=%async_computation.31 | async-start | bytes 10485760 | tf_op jit(solution)/shard_map/reduce_scatter | solution.py:265
  1098.6 369.9 %reduce-scatter.22.cloned.1.call-start = ((), (), s32[]{:S(2)}) async-start(), calls=%async_computation.27 | async-start | bytes 2621440 | tf_op jit(solution)/shard_map/reduce_scatter | solution.py:341
  1103.5 5.2 copy-start.20
  1103.5 399.1 %reduce-scatter.20.cloned.1.call-start = ((), (), s32[]{:S(2)}) async-start(), calls=%async_computation.26 | async-start | bytes 2621440 | tf_op jit(solution)/shard_map/reduce_scatter | solution.py:340
  1108.6 428.3 %reduce-scatter.26.cloned.1.call-start = ((), (), s32[]{:S(2)}) async-start(), calls=%async_computation.29 | async-start | bytes 2621440 | tf_op jit(solution)/shard_map/reduce_scatter | solution.py:343
  1113.8 5.1 copy-start.42
  1113.8 11.6 copy-start.27
  1113.8 11.6 copy-start.28
  1113.8 12.7 copy-start.40
  1113.8 13.0 copy-start.37
  1113.9 13.0 copy-start.36
  1113.9 457.4 %reduce-scatter.24.cloned.1.call-start = ((), (), s32[]{:S(2)}) async-start(), calls=%async_computation.28 | async-start | bytes 2621440 | tf_op jit(solution)/shard_map/reduce_scatter | solution.py:342
  1125.4 10.5 copy-start.47
  1126.9 85.0 %copy-start.3 = (f32[1024,256]{1,0:T(8,128)S(1)}, f32[1024,256]{1,0:T(8,128)}, u32[]{:S(2)}) copy-start(f32[1024,256]{1,0:T(8,128)} %copy-done.2) | copy-start | bytes 3145732
  1126.9 85.0 %copy-start.31 = (f32[1024]{0:T(1024)S(1)}, f32[1024]{0:T(1024)}, u32[]{:S(2)}) copy-start(f32[1024]{0:T(1024)} %copy-done.30) | copy-start | bytes 12292
  1126.9 85.0 %copy-start.33 = (f32[1024]{0:T(1024)S(1)}, f32[1024]{0:T(1024)}, u32[]{:S(2)}) copy-start(f32[1024]{0:T(1024)} %copy-done.32) | copy-start | bytes 12292
  1135.9 99.5 %copy-start.39 = (f32[4]{0:T(128)S(1)}, f32[4]{0:T(128)}, u32[]{:S(2)}) copy-start(f32[4]{0:T(128)} %copy-done.38) | copy-start | bytes 52
  (17 other events, 34.8 us)
Sparse Core Ops, SparseCore 0:
  9.5 19.4 all-gather.16
  37.3 71.8 all-gather.12
  110.8 14.8 all-gather.14
  127.1 16.6 all-gather.18
  145.2 16.6 all-gather.20
  168.7 147.8 reduce-scatter.11
  318.2 33.5 all-gather.24
  354.4 74.6 all-gather.22
  430.7 32.6 all-gather.26
  464.7 34.4 all-gather.28
  509.9 147.8 reduce-scatter.13
  666.0 73.7 all-gather.30
  766.7 146.0 reduce-scatter.15
  945.1 71.8 all-gather.32
  1065.9 146.0 reduce-scatter.17
  1214.9 70.3 reduce-scatter.31
  1288.3 71.3 reduce-scatter.27
  1362.7 71.3 reduce-scatter.29
  1437.3 31.1 reduce-scatter.21
  1471.4 31.1 reduce-scatter.19
  1505.8 31.1 reduce-scatter.25
  1540.1 31.1 reduce-scatter.23
